TPU v7x, 256 devices: a whole 4x4x8 slice. The times are simulated.
256 devices in a mesh: row: 16 (over y, z_hi), col: 16 (over x, z_lo, core).
Axes of the slice: x: 4, y: 4, z: 8 (z_hi: 4, z_lo: 2; z = z_hi * 2 + z_lo), core: 2. Of those that a mesh axis runs over, the one named last changes fastest.
Arguments:
- contact_map: float32 [2048, 2048], P('row', 'col'), may hold values from -6 to 6
- embed_weight: bfloat16 [16, 128], replicated, may hold values from -1.5 to 1.5
- embed_bias: float32 [128], replicated, may hold values from -3 to 3
- conv_weight: bfloat16 [3, 3, 3, 128, 128], replicated, may hold values from -0.1875 to 0.1875
- conv_bias: float32 [3, 128], replicated, may hold values from -3 to 3
- mix_weight: bfloat16 [128, 128], replicated, may hold values from -0.5 to 0.5
- mix_bias: float32 [128], replicated, may hold values from -6 to 6
- proj_weight: bfloat16 [128, 256], replicated, may hold values from -1 to 1
- proj_bias: float32 [256], replicated, may hold values from -3 to 3
- up_weight: bfloat16 [256, 1024], replicated, may hold values from -0.375 to 0.375
- up_bias: float32 [1024], replicated, may hold values from -3 to 3
- down_weight: bfloat16 [1024, 256], replicated, may hold values from -0.1875 to 0.1875
- down_bias: float32 [256], replicated, may hold values from -3 to 3
Outputs:
- latents: bfloat16 [512, 256], P(('row', 'col'))
- sym: bfloat16 [512, 512, 128], P('row', 'col')
All inputs are finite; a program needn't handle non-finite values.
Results may differ from a plain program's by a relative error of at most 0.0085.
Values may be sent and summed in bfloat16 or wider, within the bound.
A program may use at most 64 MiB of HBM per device.

v0:
```python
import jax
import jax.numpy as jnp
from jax import lax
from jax.sharding import PartitionSpec as P

PATCH = 4
LAYERS = 3


def cut_along(array, dim, count):
    shape = array.shape
    blocks = array.reshape(*shape[:dim], count, shape[dim] // count, *shape[dim + 1 :])
    return jnp.moveaxis(blocks, dim, 0)


def joined_along(blocks, dim):
    shape = list(blocks.shape[1:])
    shape[dim] *= blocks.shape[0]
    return jnp.moveaxis(blocks, 0, dim).reshape(shape)


def joined_exchange(array, axis, axes, splits, concats):
    sizes = [lax.axis_size(a) for a in axes]
    blocks = cut_along(array, splits[0], sizes[0])
    blocks = jnp.moveaxis(cut_along(blocks, splits[1] + 1, sizes[1]), 0, 1)
    inside = blocks.shape[2:]
    blocks = blocks.reshape(-1, *inside)
    blocks = lax.all_to_all(blocks, axis, split_axis=0, concat_axis=0, tiled=True)
    blocks = joined_along(blocks.reshape(*sizes, *inside), concats[0] + 1)
    return joined_along(blocks, concats[1])


def with_halo(array, sides, width):
    for axis, dim in sides:
        count, length = (lax.axis_size(axis), array.shape[dim])
        up = [(i, (i + 1) % count) for i in range(count - 1)]
        down = [(j, i) for i, j in up]
        last = lax.slice_in_dim(array, length - width, length, axis=dim)
        initial = lax.slice_in_dim(array, 0, width, axis=dim)
        before = lax.ppermute(last, axis, up)
        after = lax.ppermute(initial, axis, down)
        array = jnp.concatenate([before, array, after], axis=dim)
    return array


def conv_layer(padded, weight, bias, rows, cols):
    width = padded.shape[2]
    total = jnp.zeros((rows * cols, weight.shape[3]), jnp.float32)
    for offset_a in range(3):
        for offset_b in range(3):
            window = padded[offset_a : offset_a + rows, offset_b : offset_b + cols].reshape(
                rows * cols, width
            )
            total = total + jnp.dot(
                window, weight[offset_a, offset_b], preferred_element_type=jnp.float32
            )
    return jax.nn.gelu(total + bias).reshape(rows, cols, weight.shape[3])


def mirror_strips(feat, count_row, count_col, total_cells):
    width = feat.shape[2]
    strip = lax.all_to_all(feat, "col", split_axis=0, concat_axis=1, tiled=True)
    unit = strip.shape[0]
    blocks = strip.reshape(unit, count_row, count_col, unit, width)
    moved = joined_exchange(blocks, ("row", "col"), ("row", "col"), (1, 2), (1, 2))
    mirrored = moved.transpose(3, 1, 2, 0, 4).reshape(unit, total_cells, width)
    return (strip, mirrored)


def back_to_tiles(strip_values):
    return lax.all_to_all(strip_values, "col", split_axis=1, concat_axis=0, tiled=True)


def average_pair(first, second):
    return ((first.astype(jnp.float32) + second.astype(jnp.float32)) * 0.5).astype(jnp.bfloat16)


def mixed_sums(sym, mix_weight, mix_bias):
    lead, span, width = sym.shape
    mixed = jax.nn.gelu(
        jnp.dot(sym.reshape(lead * span, width), mix_weight, preferred_element_type=jnp.float32)
        + mix_bias
    )
    return jnp.sum(mixed.reshape(lead, span, width), axis=1)


def body(
    contact_map,
    embed_weight,
    embed_bias,
    conv_weight,
    conv_bias,
    mix_weight,
    mix_bias,
    proj_weight,
    proj_bias,
    up_weight,
    up_bias,
    down_weight,
    down_bias,
):
    tile_rows = contact_map.shape[0] // PATCH
    tile_cols = contact_map.shape[1] // PATCH
    width = embed_weight.shape[1]
    grid = contact_map.reshape(tile_rows, PATCH, tile_cols, PATCH).transpose(0, 2, 1, 3)
    patches = grid.reshape(tile_rows * tile_cols, PATCH * PATCH).astype(jnp.bfloat16)
    embedded = jnp.dot(patches, embed_weight, preferred_element_type=jnp.float32) + embed_bias
    feat = embedded.astype(jnp.bfloat16).reshape(tile_rows, tile_cols, width)
    count_row = lax.axis_size("row")
    count_col = lax.axis_size("col")
    total_cells = tile_rows * count_row
    depth = LAYERS
    padded = with_halo(feat, (("row", 0), ("col", 1)), depth)
    row_anchor = lax.axis_index("row") * tile_rows - depth
    col_anchor = lax.axis_index("col") * tile_cols - depth
    current = padded
    for layer in range(LAYERS):
        margin = depth - layer - 1
        rows = tile_rows + 2 * margin
        cols = tile_cols + 2 * margin
        output = conv_layer(current, conv_weight[layer], conv_bias[layer], rows, cols).astype(
            jnp.bfloat16
        )
        if margin > 0:
            row_global = row_anchor + layer + 1 + jnp.arange(rows, dtype=jnp.int32)
            col_global = col_anchor + layer + 1 + jnp.arange(cols, dtype=jnp.int32)
            row_inside = (row_global >= 0) & (row_global < total_cells)
            col_inside = (col_global >= 0) & (col_global < total_cells)
            inside = row_inside[:, None] & col_inside[None, :]
            output = jnp.where(inside[:, :, None], output, jnp.zeros((), jnp.bfloat16))
        current = output
    feat = current
    strip, mirrored = mirror_strips(feat, count_row, count_col, total_cells)
    sym_strip = average_pair(strip, mirrored)
    summed = mixed_sums(sym_strip, mix_weight, mix_bias)
    sym_tile = back_to_tiles(sym_strip)
    pooled = (summed / total_cells).astype(jnp.bfloat16)
    latent = jnp.dot(pooled, proj_weight, preferred_element_type=jnp.float32) + proj_bias
    hidden = jax.nn.gelu(
        jnp.dot(latent.astype(jnp.bfloat16), up_weight, preferred_element_type=jnp.float32)
        + up_bias
    ).astype(jnp.bfloat16)
    result = latent + jnp.dot(hidden, down_weight, preferred_element_type=jnp.float32) + down_bias
    return (result.astype(jnp.bfloat16), sym_tile)


def solution(mesh):
    return jax.shard_map(
        body,
        mesh=mesh,
        in_specs=(P("row", "col"), P(), P(), P(), P(), P(), P(), P(), P(), P(), P(), P(), P()),
        out_specs=(P(("row", "col"), None), P("row", "col", None)),
        check_vma=False,
    )
```

profile of v0, /device:TPU:1, one launch (start us, length us, event | category | flops | bytes accessed | tf_op | source)
XLA Modules:
  0.0 107.0 jit_solution(87981411836727438)
XLA Ops:
  0.6 0.9 convert_element_type.87
  1.5 2.2 %convert_element_type.88 = bf16[32,4,32,4]{3,2,1,0:T(8,128)(2,1)S(1)} reshape(bf16[128,128]{1,0:T(8,128)(2,1)S(1)} %convert_element_type.87) | data formatting | bytes 65536 | tf_op jit(solution)/shard_map/convert_element_type | solution.py:106
  3.8 1.0 copy.24
  5.8 1.3 %collective-permute-start.1 = (bf16[3,32,128]{2,1,0:T(8,128)(2,1)S(1)}, bf16[3,32,128]{2,1,0:T(8,128)(2,1)S(1)}, u32[]{:S(2)}, u32[]{:S(2)}) collective-permute-start(bf16[3,32,128]{2,1,0:T(8,128)(2,1)S(1)} %bitcast.213), channel_id=1, source_target_pairs={{16,0},{32,16},{48,32},{64,48},{80,64},{96,80},{112,96},{128,112},... | collective-permute-start | bytes 73736 | tf_op jit(solution)/shard_map/ppermute | solution.py:41
  7.1 6.3 %collective-permute-start = (bf16[3,32,128]{2,1,0:T(8,128)(2,1)S(1)}, bf16[3,32,128]{2,1,0:T(8,128)(2,1)S(1)}, u32[]{:S(2)}, u32[]{:S(2)}) collective-permute-start(bf16[3,32,128]{2,1,0:T(8,128)(2,1)S(1)} %bitcast.212), channel_id=1, source_target_pairs={{0,16},{16,32},{32,48},{48,64},{64,80},{80,96},{96,112},{112,128},... | collective-permute-start | bytes 73736 | tf_op jit(solution)/shard_map/ppermute | solution.py:40
  13.4 1.0 slice_bitcast_fusion
  15.3 4.4 %collective-permute-start.2 = (bf16[38,3,128]{2,1,0:T(4,128)(2,1)S(1)}, bf16[38,3,128]{2,1,0:T(4,128)(2,1)S(1)}, u32[]{:S(2)}, u32[]{:S(2)}) collective-permute-start(bf16[38,3,128]{2,1,0:T(4,128)(2,1)S(1)} %get-tuple-element.32), channel_id=1, source_target_pairs={{0,1},{1,2},{2,3},{3,4},{4,5},{5,6},{6,7},{7,8},{8,9},{9,10},{10,1... | collective-permute-start | bytes 87560 | tf_op jit(solution)/shard_map/ppermute | solution.py:40
  19.6 1.9 %collective-permute-start.3 = (bf16[38,3,128]{2,1,0:T(4,128)(2,1)S(1)}, bf16[38,3,128]{2,1,0:T(4,128)(2,1)S(1)}, u32[]{:S(2)}, u32[]{:S(2)}) collective-permute-start(bf16[38,3,128]{2,1,0:T(4,128)(2,1)S(1)} %get-tuple-element.33), channel_id=1, source_target_pairs={{1,0},{2,1},{3,2},{4,3},{5,4},{6,5},{7,6},{8,7},{9,8},{10,9},{11,1... | collective-permute-start | bytes 87560 | tf_op jit(solution)/shard_map/ppermute | solution.py:41
  22.2 2.8 %collective-permute-done.3 = bf16[38,3,128]{2,1,0:T(4,128)(2,1)S(1)} collective-permute-done((bf16[38,3,128]{2,1,0:T(4,128)(2,1)S(1)}, bf16[38,3,128]{2,1,0:T(4,128)(2,1)S(1)}, u32[]{:S(2)}, u32[]{:S(2)}) %collective-permute-start.3) | collective-permute-done | bytes 29216 | tf_op jit(solution)/shard_map/ppermute | solution.py:41
  25.1 1.2 %fusion.65 = (bf16[36,36,128]{2,1,0:T(8,128)(2,1)}, bf16[36,36,128]{2,1,0:T(8,128)(2,1)S(1)}, bf16[36,36,128]{2,1,0:T(8,128)(2,1)S(1)}, bf16[36,36,128]{2,1,0:T(...) fusion(bf16[38,38,128]{2,1,0:T(8,128)(2,1)S(1)} %pad_maximum_fusion), kind=kLoop, calls=%fused_computation.149 | loop fusion | bytes 5971968 | tf_op jit(solution)/shard_map/slice | solution.py:51
  26.3 1.8 %reshape.229 = bf16[1296,128]{1,0:T(8,128)(2,1)} reshape(bf16[36,36,128]{2,1,0:T(8,128)(2,1)} %get-tuple-element.5) | data formatting | bytes 663552 | tf_op jit(solution)/shard_map/reshape | solution.py:51
  29.4 1.1 %fusion.43 = f32[1296,128]{1,0:T(8,128)S(1)} fusion(bf16[1296,128]{1,0:T(8,128)(2,1)S(1)} %reshape.222, bf16[3,3,128,128]{3,2,1,0:T(8,128)(2,1)} %get-tuple-element.3), kind=kOutput, calls=%fused_computation.116 | convolution fusion | flops 42467328 | bytes 1028096 | tf_op jit(solution)/shard_map/dot_general | solution.py:54
  34.8 1.1 %fusion.66 = (bf16[34,34,128]{2,1,0:T(8,128)(2,1)}, bf16[34,34,128]{2,1,0:T(8,128)(2,1)S(1)}, bf16[34,34,128]{2,1,0:T(8,128)(2,1)S(1)}, bf16[34,34,128]{2,1,0:T(...) fusion(bf16[36,36,128]{2,1,0:T(8,128)(2,1)S(1)} %broadcast_sele, ...), kind=kLoop, calls=%fused_computation.150 | loop fusion | bytes 5326848 | tf_op jit(solution)/shard_map/slice | solution.py:51
  36.0 1.8 %reshape.238 = bf16[1156,128]{1,0:T(8,128)(2,1)} reshape(bf16[34,34,128]{2,1,0:T(8,128)(2,1)} %get-tuple-element.14) | data formatting | bytes 591872 | tf_op jit(solution)/shard_map/reshape | solution.py:51
  37.8 0.8 reshape.237
  39.3 0.9 copy-done.3
  48.9 12.5 %all_to_all.38 = bf16[32,32,128]{2,1,0:T(8,128)(2,1)S(1)} all-to-all(bf16[32,32,128]{2,1,0:T(8,128)(2,1)S(1)} %bitcast.211), channel_id=1, replica_groups=mesh['row'=16,'col'=16] {'col'}, dimensions={0} | all-to-all | bytes 524288 | tf_op jit(solution)/shard_map/all_to_all | solution.py:62
  61.5 1.1 %copy.26 = bf16[2,16,1,16,2,128]{5,0,4,3,1,2:T(2,128)(2,1)} copy(bf16[2,16,1,16,2,128]{5,4,3,1,0,2:T(2,128)(2,1)S(1)} %bitcast.208) | data formatting | bytes 524288 | tf_op jit(solution)/shard_map/reshape;reshape | solution.py:12
  62.6 14.4 %all-to-all-start.1 = ((bf16[256,2,1,1,2,128]{5,1,4,3,2,0:T(2,128)(2,1)}), bf16[256,2,1,1,2,128]{5,1,4,3,2,0:T(2,128)(2,1)S(1)}, u32[]{:S(2)}, u32[]{:S(2)}) async-start(bf16[256,2,1,1,2,128]{5,1,4,3,2,0:T(2,128)(2,1)} %bitcast.54), calls=%async_computation.1 | async-start | bytes 524288 | tf_op jit(solution)/shard_map/all_to_all | solution.py:28
  77.4 15.3 %all-to-all-done.1 = bf16[256,2,1,1,2,128]{5,1,4,3,2,0:T(2,128)(2,1)S(1)} async-done(((bf16[256,2,1,1,2,128]{5,1,4,3,2,0:T(2,128)(2,1)}), bf16[256,2,1,1,2,128]{5,1,4,3,2,0:T(2,128)(2,1)S(1)}, u32[]{:S(2)}, u32[]{:S(2)}) %all-to-all-start.1) | async-done | bytes 262176 | tf_op jit(solution)/shard_map/all_to_all | solution.py:28
  93.7 1.1 %fusion.38 = bf16[2,512,128]{2,0,1:T(2,128)(2,1)} fusion(f32[2,16,16,2,128]{4,0,3,2,1:T(2,128)S(1)} %copy.29, f32[2,16,32,128]{3,0,2,1:T(2,128)S(1)} %copy.28), kind=kLoop, calls=%fused_computation.72 | loop fusion | flops 393216 | bytes 1310720 | tf_op jit(solution)/shard_map/convert_element_type | solution.py:75
  94.9 4.1 %all-to-all-start.2 = ((bf16[2,512,128]{2,0,1:T(2,128)(2,1)}), bf16[2,512,128]{2,0,1:T(2,128)(2,1)S(1)}, u32[]{:S(2)}, u32[]{:S(2)}) async-start(bf16[2,512,128]{2,0,1:T(2,128)(2,1)} %fusion.38), calls=%async_computation.2 | async-start | bytes 524288 | tf_op jit(solution)/shard_map/all_to_all | solution.py:71
  100.6 0.9 fusion.5
  101.5 4.7 %all-to-all-done.2 = bf16[2,512,128]{2,0,1:T(2,128)(2,1)S(1)} async-done(((bf16[2,512,128]{2,0,1:T(2,128)(2,1)}), bf16[2,512,128]{2,0,1:T(2,128)(2,1)S(1)}, u32[]{:S(2)}, u32[]{:S(2)}) %all-to-all-start.2) | async-done | bytes 262176 | tf_op jit(solution)/shard_map/all_to_all | solution.py:71
  (112 shorter events, 21.1 us)
Async XLA Ops:
  0.6 99.3 %copy-start = (bf16[1024,256]{1,0:T(8,128)(2,1)S(1)}, bf16[1024,256]{1,0:T(8,128)(2,1)}, u32[]{:S(2)}) copy-start(bf16[1024,256]{1,0:T(8,128)(2,1)} %param.24) | copy-start | bytes 1572868
  3.8 9.6 %copy-start.6 = (bf16[3,3,3,128,128]{4,3,2,1,0:T(8,128)(2,1)S(1)}, bf16[3,3,3,128,128]{4,3,2,1,0:T(8,128)(2,1)}, u32[]{:S(2)}) copy-start(bf16[3,3,3,128,128]{4,3,2,1,0:T(8,128)(2,1)} %param.16) | copy-start | bytes 2654212
  4.8 0.7 copy-start.12
  5.8 9.4 %collective-permute-start.1 = (bf16[3,32,128]{2,1,0:T(8,128)(2,1)S(1)}, bf16[3,32,128]{2,1,0:T(8,128)(2,1)S(1)}, u32[]{:S(2)}, u32[]{:S(2)}) collective-permute-start(bf16[3,32,128]{2,1,0:T(8,128)(2,1)S(1)} %bitcast.213), channel_id=1, source_target_pairs={{16,0},{32,16},{48,32},{64,48},{80,64},{96,80},{112,96},{128,112},... | collective-permute-start | bytes 73736 | tf_op jit(solution)/shard_map/ppermute | solution.py:41
  7.1 8.1 %collective-permute-start = (bf16[3,32,128]{2,1,0:T(8,128)(2,1)S(1)}, bf16[3,32,128]{2,1,0:T(8,128)(2,1)S(1)}, u32[]{:S(2)}, u32[]{:S(2)}) collective-permute-start(bf16[3,32,128]{2,1,0:T(8,128)(2,1)S(1)} %bitcast.212), channel_id=1, source_target_pairs={{0,16},{16,32},{32,48},{48,64},{64,80},{80,96},{96,112},{112,128},... | collective-permute-start | bytes 73736 | tf_op jit(solution)/shard_map/ppermute | solution.py:40
  15.2 6.3 %copy-start.14 = (f32[3,128]{1,0:T(4,128)S(1)}, f32[3,128]{1,0:T(4,128)}, u32[]{:S(2)}) copy-start(f32[3,128]{1,0:T(4,128)} %param.17) | copy-start | bytes 4612
  15.3 6.9 %collective-permute-start.2 = (bf16[38,3,128]{2,1,0:T(4,128)(2,1)S(1)}, bf16[38,3,128]{2,1,0:T(4,128)(2,1)S(1)}, u32[]{:S(2)}, u32[]{:S(2)}) collective-permute-start(bf16[38,3,128]{2,1,0:T(4,128)(2,1)S(1)} %get-tuple-element.32), channel_id=1, source_target_pairs={{0,1},{1,2},{2,3},{3,4},{4,5},{5,6},{6,7},{7,8},{8,9},{9,10},{10,1... | collective-permute-start | bytes 87560 | tf_op jit(solution)/shard_map/ppermute | solution.py:40
  19.6 5.3 %collective-permute-start.3 = (bf16[38,3,128]{2,1,0:T(4,128)(2,1)S(1)}, bf16[38,3,128]{2,1,0:T(4,128)(2,1)S(1)}, u32[]{:S(2)}, u32[]{:S(2)}) collective-permute-start(bf16[38,3,128]{2,1,0:T(4,128)(2,1)S(1)} %get-tuple-element.33), channel_id=1, source_target_pairs={{1,0},{2,1},{3,2},{4,3},{5,4},{6,5},{7,6},{8,7},{9,8},{10,9},{11,1... | collective-permute-start | bytes 87560 | tf_op jit(solution)/shard_map/ppermute | solution.py:41
  29.4 1.1 %copy-start.4 = (bf16[3,3,128,128]{3,2,1,0:T(8,128)(2,1)S(1)}, bf16[3,3,128,128]{3,2,1,0:T(8,128)(2,1)}, u32[]{:S(2)}) copy-start(bf16[3,3,128,128]{3,2,1,0:T(8,128)(2,1)} %get-tuple-element.3) | copy-start | bytes 884740
  32.1 1.0 copy-start.1
  33.1 1.0 copy-start.8
  39.2 1.0 copy-start.3
  41.9 1.0 copy-start.2
  42.9 1.0 copy-start.9
  45.2 1.0 copy-start.5
  62.6 30.1 %all-to-all-start.1 = ((bf16[256,2,1,1,2,128]{5,1,4,3,2,0:T(2,128)(2,1)}), bf16[256,2,1,1,2,128]{5,1,4,3,2,0:T(2,128)(2,1)S(1)}, u32[]{:S(2)}, u32[]{:S(2)}) async-start(bf16[256,2,1,1,2,128]{5,1,4,3,2,0:T(2,128)(2,1)} %bitcast.54), calls=%async_computation.1 | async-start | bytes 524288 | tf_op jit(solution)/shard_map/all_to_all | solution.py:28
  94.9 4.1 %copy-start.20 = (bf16[128,128]{1,0:T(8,128)(2,1)S(1)}, bf16[128,128]{1,0:T(8,128)(2,1)}, u32[]{:S(2)}) copy-start(bf16[128,128]{1,0:T(8,128)(2,1)} %param.18) | copy-start | bytes 98308
  94.9 4.1 %copy-start.21 = (f32[128]{0:T(128)S(1)}, f32[128]{0:T(128)}, u32[]{:S(2)}) copy-start(f32[128]{0:T(128)} %param.19) | copy-start | bytes 1540
  94.9 11.4 %all-to-all-start.2 = ((bf16[2,512,128]{2,0,1:T(2,128)(2,1)}), bf16[2,512,128]{2,0,1:T(2,128)(2,1)S(1)}, u32[]{:S(2)}, u32[]{:S(2)}) async-start(bf16[2,512,128]{2,0,1:T(2,128)(2,1)} %fusion.38), calls=%async_computation.2 | async-start | bytes 524288 | tf_op jit(solution)/shard_map/all_to_all | solution.py:71
  99.0 0.8 copy-start.10
  99.0 0.8 copy-start.15
  99.0 1.1 copy-start.7
  99.8 0.7 copy-start.13
  99.8 0.7 copy-start.16
  (4 other events, 2.7 us)
where the time goes:
time: 108 us; the launch traced here: 107 us
  starting transfers between devices  32.4 us (30%)
  local copies, waits for them, and re-layouts  23.9 us (22%)
  waiting for transfers between devices  22.8 us (21%)
  blocking collectives  12.5 us (12%)
  matrix products  10.2 us (9%)
  other arithmetic  3.86 us (4%)
  between operations  1.23 us (1%)
    all_to_all x1, waiting for transfers between devices, joined_exchange(): lax.all_to_all(blocks, axis, split_axis=0, concat_axis=0, tiled=True)  15.3 us
    all_to_all x1, starting transfers between devices, joined_exchange(): lax.all_to_all(blocks, axis, split_axis=0, concat_axis=0, tiled=True)  14.4 us
    all_to_all x1, blocking collectives, mirror_strips(): strip = lax.all_to_all(feat, 'col', split_axis=0, concat_axis=1, tiled=True)  12.5 us
    ppermute x2, starting transfers between devices, with_halo(): before = lax.ppermute(last, axis, up)  10.7 us
    dot_general x27, matrix products, conv_layer(): jnp.dot(window, weight[offset_a, offset_b], preferred_element_type=jnp.fl...  8.52 us
    unnamed x44, local copies, waits for them, and re-layouts  7 us
    reshape x18, local copies, waits for them, and re-layouts, conv_layer(): padded[offset_a:offset_a + rows, offset_b:offset_b + cols]  6.26 us
    all_to_all x1, waiting for transfers between devices, back_to_tiles(): lax.all_to_all(strip_values, 'col', split_axis=1, concat_axis=0, tiled=True)  4.72 us
  transfers between devices with their start and end apart: 6, of which 3 were waited for; matrix products, arithmetic and copies ran while one was open for 4% of the time, Pallas kernels for 0%

commit v1 on v0

v1 whole, which is shorter than its diff:
```python
import functools

import jax
import jax.numpy as jnp
from jax import lax
from jax.experimental import pallas as pl
from jax.experimental.pallas import tpu as pltpu
from jax.sharding import PartitionSpec as P

PATCH = 4
LAYERS = 3
TILE = 32
BLK = 8
PAD = 16
SUB = 48
CH = 128
MESH = pl.DeviceIdType.MESH
F32 = jnp.float32
BF16 = jnp.bfloat16
OFFSETS = [(dl, ds) for dl in (-1, 0, 1) for ds in (-1, 0, 1)]


def gelu(x):
    half = 0.5 * x
    inner = x * (0.7978845608028654 + (0.7978845608028654 * 0.044715) * (x * x))
    return half + half * jnp.tanh(inner)


def lead_src(d):
    return {-1: pl.ds(3, 1), 0: pl.ds(0, 4), 1: pl.ds(0, 1)}[d]


def lead_dst(d):
    return {-1: pl.ds(0, 1), 0: pl.ds(1, 4), 1: pl.ds(5, 1)}[d]


def sub_src(d):
    return {-1: pl.ds(TILE - PAD, PAD), 0: pl.ds(0, TILE), 1: pl.ds(0, PAD)}[d]


def sub_dst(d):
    return {-1: pl.ds(0, PAD), 0: pl.ds(PAD, TILE), 1: pl.ds(PAD + TILE, PAD)}[d]


def kernel(
    n,
    x_ref,
    ew_ref,
    eb_ref,
    cw_hbm,
    cb_ref,
    mw_ref,
    mb_ref,
    pw_hbm,
    pb_ref,
    uw_hbm,
    ub_ref,
    dw_hbm,
    db_ref,
    lat_ref,
    sym_hbm,
    xt,
    own_p,
    own_q,
    near_h,
    far_h,
    f0,
    f1,
    f2,
    f3,
    symb,
    cw,
    pw,
    uw,
    dw,
    part,
    got,
    near_ss,
    near_rs,
    far_ss,
    far_rs,
    red_ss,
    red_rs,
    wsem,
    osem,
):
    r = lax.axis_index("row")
    c = lax.axis_index("col")
    rows_each = TILE // n

    weights = [
        pltpu.make_async_copy(src, dst, wsem.at[k])
        for k, (src, dst) in enumerate([(cw_hbm, cw), (pw_hbm, pw), (uw_hbm, uw), (dw_hbm, dw)])
    ]
    for w in weights:
        w.start()

    def inside(a, b):
        return (a >= 0) & (a < n) & (b >= 0) & (b < n)

    barrier = pltpu.get_barrier_semaphore()
    count = jnp.int32(n - 1)

    def greet(a, b):
        pl.semaphore_signal(barrier, inc=1, device_id=(a, b), device_id_type=MESH)

    for dl, ds in OFFSETS:
        far_ok = inside(c + ds, r + dl) & ((c + ds != r) | (r + dl != c))
        pl.when(far_ok)(functools.partial(greet, c + ds, r + dl))
        count += far_ok.astype(jnp.int32)
    for dl, ds in OFFSETS:
        if dl or ds:
            near_ok = inside(r + dl, c + ds)
            pl.when(near_ok)(functools.partial(greet, r + dl, c + ds))
            count += near_ok.astype(jnp.int32)
    for k in range(1, n):
        greet(r, lax.rem(c + k, n))

    xt[...] = x_ref[...].T
    y_p = jnp.concatenate([x_ref[pl.ds(s, TILE, stride=PATCH), :] for s in range(PATCH)], axis=1)
    y_q = jnp.concatenate([xt[pl.ds(s, TILE, stride=PATCH), :] for s in range(PATCH)], axis=1)
    y = jnp.concatenate([y_p, y_q], axis=0).astype(BF16)
    k = lax.broadcasted_iota(jnp.int32, (512, 512), 0)
    target = ((k >> 5) & 3) * 128 + ((k >> 2) & 7) * 16 + (k >> 7) * 4 + (k & 3)
    perm = (lax.broadcasted_iota(jnp.int32, (512, 512), 1) == target).astype(F32).astype(BF16)
    z = jnp.dot(y, perm, preferred_element_type=F32).astype(BF16)
    for h in range(4):
        p_h = z[:TILE, h * 128 : (h + 1) * 128]
        q_h = z[TILE:, h * 128 : (h + 1) * 128]
        own_p[h] = p_h
        own_q[h] = q_h
        near_h[h + 1, PAD : PAD + TILE, :] = q_h

    pr = lax.broadcasted_iota(jnp.int32, (128, 16), 0)
    pc = lax.broadcasted_iota(jnp.int32, (128, 16), 1)
    rid = lax.broadcasted_iota(jnp.int32, (128, 128), 0) >> 4

    def block_diagonal(swap):
        row = (pr & 3) * 4 + ((pr >> 2) & 3) if swap else pr & 15
        pick = (pc == row).astype(F32).astype(BF16)
        tiled = jnp.dot(pick, ew_ref[...], preferred_element_type=F32)
        return jnp.concatenate(
            [jnp.where(rid == b, tiled, 0.0).astype(BF16) for b in range(BLK)], axis=1
        )

    pl.semaphore_wait(barrier, count)

    def message(src, dst, ss, rs, dl, ds, a, b):
        i = (dl + 1) * 3 + ds + 1
        return pltpu.make_async_remote_copy(
            src_ref=src.at[lead_src(dl), sub_src(ds), :],
            dst_ref=dst.at[lead_dst(dl), sub_dst(ds), :],
            send_sem=ss.at[i],
            recv_sem=rs.at[i],
            device_id=(a, b),
            device_id_type=MESH,
        )

    far_out, far_in, near_out, near_in = [], [], [], []
    for dl, ds in OFFSETS:
        a, b = c - dl, r - ds
        ok = inside(a, b) & ((a != r) | (b != c))
        out = message(own_p, far_h, far_ss, far_rs, dl, ds, a, b)
        far_out.append((ok, out))
        pl.when(ok)(out.start)
        ok_in = inside(c + ds, r + dl) & ((c + ds != r) | (r + dl != c))
        far_in.append((ok_in, message(own_p, far_h, far_ss, far_rs, dl, ds, r, c)))
    for dl, ds in OFFSETS:
        if dl or ds:
            a, b = r - dl, c - ds
            ok = inside(a, b)
            out = message(own_q, near_h, near_ss, near_rs, dl, ds, a, b)
            near_out.append((ok, out))
            pl.when(ok)(out.start)
            near_in.append(
                (inside(r + dl, c + ds), message(own_q, near_h, near_ss, near_rs, dl, ds, r, c))
            )

    def keep(dl, ds):
        far_h[lead_dst(dl), sub_dst(ds), :] = own_p[lead_src(dl), sub_src(ds), :]

    pl.when(r == c)(functools.partial(keep, 0, 0))
    pl.when(c == r + 1)(functools.partial(keep, 1, -1))
    pl.when(c == r - 1)(functools.partial(keep, -1, 1))

    sub_cell = c * TILE - 8 + lax.broadcasted_iota(jnp.int32, (1, SUB, 1), 1)
    sub_ok = (sub_cell >= 0) & (sub_cell < n * TILE)

    def masked(value, first):
        count_l = value.shape[0]
        lead = r * TILE + first + lax.broadcasted_iota(jnp.int32, (count_l, SUB, 1), 0)
        ok = sub_ok & (lead >= 0) & (lead < n * TILE)
        return jnp.where(ok, value, 0.0)

    def put(ref, at, value, cut=False):
        count_l = value.shape[0]
        flat = value.reshape(count_l * SUB, CH)
        for s in range(3):
            moved = flat if s == 1 else pltpu.roll(flat, 1 if s == 0 else count_l * SUB - 1, 0)
            moved = moved.reshape(count_l, SUB, CH)
            if cut:
                moved = moved[:, 8:40, :]
            ref[s, at : at + count_l] = moved.astype(BF16)

    def embed(patches, diag):
        for h in range(6):
            first, last = (5, 8) if h == 0 else (0, 3) if h == 5 else (0, 8)
            wide = jnp.dot(patches[h], diag, preferred_element_type=F32)
            cells = jnp.concatenate(
                [
                    (wide[8:56, b * CH : (b + 1) * CH] + eb_ref[...])[None]
                    for b in range(first, last)
                ],
                axis=0,
            )
            at = h * BLK + first - 5
            put(f0, at, masked(cells, at - 3))

    def conv(layer, src, at, count_l, lead_is_row):
        pieces = []
        for a in range(3):
            for b in range(3):
                lead, sub = (a, b) if lead_is_row else (b, a)
                piece = src[sub, at + lead : at + lead + count_l]
                pieces.append(piece.reshape(count_l * piece.shape[1], CH))
        lhs = jnp.concatenate(pieces, axis=1)
        total = jnp.dot(lhs, cw[layer], preferred_element_type=F32)
        return gelu(total + cb_ref[layer])

    def features(lead_is_row, finish):
        for at in range(0, 36, 12):
            v = conv(0, f0, at, 12, lead_is_row).reshape(12, SUB, CH)
            put(f1, at, masked(v, at - 2))
        for at in range(0, 34, 17):
            v = conv(1, f1, at, 17, lead_is_row).reshape(17, SUB, CH)
            put(f2, at, masked(v, at - 1), cut=True)
        for at in range(0, TILE, 16):
            finish(at, conv(2, f2, at, 16, lead_is_row).astype(BF16))

    diag_q = block_diagonal(True)
    for ok, got_in in near_in:
        pl.when(ok)(got_in.wait_recv)
    embed(near_h, diag_q)
    weights[0].wait()

    def keep_own(at, value):
        f3[at * TILE : (at + 16) * TILE, :] = value

    features(True, keep_own)

    diag_p = block_diagonal(False)
    for ok, got_in in far_in:
        pl.when(ok)(got_in.wait_recv)
    embed(far_h, diag_p)

    outs = []

    def finish_far(at, value):
        mean = (f3[at * TILE : (at + 16) * TILE, :].astype(F32) + value.astype(F32)) * 0.5
        sym = mean.astype(BF16)
        symb[at : at + 16] = sym.reshape(16, TILE, CH)
        out = pltpu.make_async_copy(symb.at[pl.ds(at, 16)], sym_hbm.at[pl.ds(at, 16)], osem.at[at // 16])
        out.start()
        outs.append(out)
        mixed = gelu(jnp.dot(sym, mw_ref[...], preferred_element_type=F32) + mb_ref[...])
        sums = jnp.sum(mixed.reshape(16, TILE, CH), axis=1)
        for g in range(16 // rows_each):
            part[at // rows_each + g] = sums[g * rows_each : (g + 1) * rows_each]

    features(False, finish_far)

    moves = []
    for k in range(1, n):
        to = lax.rem(c + k, n)
        move = pltpu.make_async_remote_copy(
            src_ref=part.at[to],
            dst_ref=got.at[k],
            send_sem=red_ss.at[k],
            recv_sem=red_rs.at[k],
            device_id=(r, to),
            device_id_type=MESH,
        )
        move.start()
        moves.append(move)
    for w in weights[1:]:
        w.wait()
    for move in moves:
        move.wait_recv()
    summed = part[c]
    for k in range(1, n):
        summed = summed + got[k]
    pooled = (summed / (n * TILE)).astype(BF16)
    latent = jnp.dot(pooled, pw[...], preferred_element_type=F32) + pb_ref[...]
    hidden = gelu(jnp.dot(latent.astype(BF16), uw[...], preferred_element_type=F32) + ub_ref[...])
    result = latent + jnp.dot(hidden.astype(BF16), dw[...], preferred_element_type=F32) + db_ref[...]
    lat_ref[...] = result.astype(BF16)

    for move in moves:
        move.wait_send()
    for ok, out in far_out + near_out:
        pl.when(ok)(out.wait_send)
    for out in outs:
        out.wait()


def body(
    contact_map,
    embed_weight,
    embed_bias,
    conv_weight,
    conv_bias,
    mix_weight,
    mix_bias,
    proj_weight,
    proj_bias,
    up_weight,
    up_bias,
    down_weight,
    down_bias,
):
    n = lax.axis_size("col")
    rows_each = TILE // n
    latent_width, hidden_width = up_weight.shape
    vmem = pl.BlockSpec(memory_space=pltpu.VMEM)
    hbm = pl.BlockSpec(memory_space=pl.ANY)
    dma = pltpu.SemaphoreType.DMA
    return pl.pallas_call(
        functools.partial(kernel, n),
        out_shape=(
            jax.ShapeDtypeStruct((rows_each, latent_width), BF16),
            jax.ShapeDtypeStruct((TILE, TILE, CH), BF16),
        ),
        in_specs=[vmem, vmem, vmem, hbm, vmem, vmem, vmem, hbm, vmem, hbm, vmem, hbm, vmem],
        out_specs=(vmem, hbm),
        scratch_shapes=[
            pltpu.VMEM((TILE * PATCH, TILE * PATCH), F32),
            pltpu.VMEM((4, TILE, 128), BF16),
            pltpu.VMEM((4, TILE, 128), BF16),
            pltpu.VMEM((6, TILE + 2 * PAD, 128), BF16),
            pltpu.VMEM((6, TILE + 2 * PAD, 128), BF16),
            pltpu.VMEM((3, 38, SUB, CH), BF16),
            pltpu.VMEM((3, 36, SUB, CH), BF16),
            pltpu.VMEM((3, 34, TILE, CH), BF16),
            pltpu.VMEM((TILE * TILE, CH), BF16),
            pltpu.VMEM((TILE, TILE, CH), BF16),
            pltpu.VMEM((LAYERS, 9 * CH, CH), BF16),
            pltpu.VMEM(proj_weight.shape, BF16),
            pltpu.VMEM(up_weight.shape, BF16),
            pltpu.VMEM(down_weight.shape, BF16),
            pltpu.VMEM((n, rows_each, CH), F32),
            pltpu.VMEM((n, rows_each, CH), F32),
            dma((9,)),
            dma((9,)),
            dma((9,)),
            dma((9,)),
            dma((n,)),
            dma((n,)),
            dma((4,)),
            dma((2,)),
        ],
        compiler_params=pltpu.CompilerParams(
            collective_id=0, has_side_effects=True, vmem_limit_bytes=48 * 1024 * 1024
        ),
    )(
        contact_map,
        embed_weight,
        embed_bias.reshape(1, CH),
        conv_weight.reshape(LAYERS, 9 * CH, CH),
        conv_bias.reshape(LAYERS, 1, CH),
        mix_weight,
        mix_bias.reshape(1, CH),
        proj_weight,
        proj_bias.reshape(1, latent_width),
        up_weight,
        up_bias.reshape(1, hidden_width),
        down_weight,
        down_bias.reshape(1, latent_width),
    )


def solution(mesh):
    return jax.shard_map(
        body,
        mesh=mesh,
        in_specs=(P("row", "col"),) + (P(),) * 12,
        out_specs=(P(("row", "col"), None), P("row", "col", None)),
        check_vma=False,
    )
```

time: 108 us -> 40.3 us (0.37)
  starting transfers between devices: 32.4 us -> 0 us
  Pallas kernels: 0 us -> 30.9 us
  waiting for transfers between devices: 22.8 us -> 0 us
  local copies, waits for them, and re-layouts: 23.9 us -> 8.26 us
  blocking collectives: 12.5 us -> 0 us
  matrix products: 10.2 us -> 0 us
  other arithmetic: 3.86 us -> 0 us
    pallas_call x0 -> x1, Pallas kernels: none -> 30.9 us  [body(): pl.pallas_call(functools.partial(kernel, n), out_shape=(jax.ShapeDtypeStr...]
    all_to_all x2 -> x0, waiting for transfers between devices: 20 us -> none  [the longest x1 15.3 us: joined_exchange(): lax.all_to_all(blocks, axis, split_axis=0, concat_axis=0, tiled=True)]
    all_to_all x2 -> x0, starting transfers between devices: 18.5 us -> none  [the longest x1 14.4 us: joined_exchange(): lax.all_to_all(blocks, axis, split_axis=0, concat_axis=0, tiled=True)]
    ppermute x4 -> x0, starting transfers between devices: 13.9 us -> none  [the longest x2 10.7 us: with_halo(): before = lax.ppermute(last, axis, up)]
    all_to_all x1 -> x0, blocking collectives: 12.5 us -> none  [mirror_strips(): strip = lax.all_to_all(feat, 'col', split_axis=0, concat_axis=1, tiled=True)]
    dot_general x31 -> x0, matrix products: 10.2 us -> none  [the longest x27 8.52 us: conv_layer(): jnp.dot(window, weight[offset_a, offset_b], preferred_element_type=jnp.fl...]
    reshape x18 -> x1, local copies, waits for them, and re-layouts: 6.26 us -> 0.01 us  [body(): conv_bias.reshape(LAYERS, 1, CH)]
    convert_element_type x8 -> x0, local copies, waits for them, and re-layouts: 4.61 us -> none  [the longest x3 3.39 us: body(): grid.reshape(tile_rows * tile_cols, PATCH * PATCH).astype(jnp.bfloat16)]
  transfers between devices with their start and end apart: 6 -> 0, of which waited for: 3 -> 0; matrix products, arithmetic and copies ran while one was open for 4% -> 0% of each run, Pallas kernels for 0% -> 0%
where the time goes in v1:
time: 40.3 us; the launch traced here: 39.9 us
  Pallas kernels  30.9 us (77%)
  local copies, waits for them, and re-layouts  8.26 us (20%)
  between operations  0.7 us (2%)
    pallas_call x1, Pallas kernels, body(): pl.pallas_call(functools.partial(kernel, n), out_shape=(jax.ShapeDtypeStr...  30.9 us
    unnamed x28, local copies, waits for them, and re-layouts  8.26 us

profile of v1, /device:TPU:1, one launch (start us, length us, event | category | flops | bytes accessed | tf_op | source)
XLA Modules:
  0.0 39.9 jit_solution(9088299390843251499)
XLA Ops:
  0.6 0.0 copy-start.12
  0.6 0.0 copy-start.9
  0.7 0.0 copy-start.10
  0.7 0.0 copy-start.11
  0.7 0.0 copy-start.7
  0.7 0.0 copy-start.6
  0.7 0.6 %copy-done.12 = f32[3,128]{1,0:T(4,128)S(1)} copy-done((f32[3,128]{1,0:T(4,128)S(1)}, f32[3,128]{1,0:T(4,128)}, u32[]{:S(2)}) %copy-start.12) | copy-done | bytes 1560
  1.3 0.0 copy-start.8
  1.3 0.0 copy-done.9
  1.3 0.0 copy-done.10
  1.3 0.0 copy-done.11
  1.3 0.0 copy-done.7
  1.4 0.0 copy-done.6
  1.4 0.6 %copy-done.8 = f32[256]{0:T(256)S(1)} copy-done((f32[256]{0:T(256)S(1)}, f32[256]{0:T(256)}, u32[]{:S(2)}) %copy-start.8) | copy-done | bytes 1048
  2.0 0.0 copy-start
  2.0 1.2 %copy-done = bf16[3,3,3,128,128]{4,3,2,1,0:T(8,128)(2,1)S(1)} copy-done((bf16[3,3,3,128,128]{4,3,2,1,0:T(8,128)(2,1)S(1)}, bf16[3,3,3,128,128]{4,3,2,1,0:T(8,128)(2,1)}, u32[]{:S(2)}) %copy-start) | copy-done | bytes 884760
  3.2 1.0 %copy-done.1 = bf16[256,1024]{1,0:T(8,128)(2,1)S(1)} copy-done((bf16[256,1024]{1,0:T(8,128)(2,1)S(1)}, bf16[256,1024]{1,0:T(8,128)(2,1)}, u32[]{:S(2)}) %copy-start.1) | copy-done | bytes 524312
  4.2 1.0 %copy-done.2 = bf16[1024,256]{1,0:T(8,128)(2,1)S(1)} copy-done((bf16[1024,256]{1,0:T(8,128)(2,1)S(1)}, bf16[1024,256]{1,0:T(8,128)(2,1)}, u32[]{:S(2)}) %copy-start.2) | copy-done | bytes 524312
  5.2 0.8 %copy-done.3 = f32[128,128]{1,0:T(8,128)S(1)} copy-done((f32[128,128]{1,0:T(8,128)S(1)}, f32[128,128]{1,0:T(8,128)}, u32[]{:S(2)}) %copy-start.3) | copy-done | bytes 65560
  6.1 0.8 %copy-done.4 = bf16[128,256]{1,0:T(8,128)(2,1)S(1)} copy-done((bf16[128,256]{1,0:T(8,128)(2,1)S(1)}, bf16[128,256]{1,0:T(8,128)(2,1)}, u32[]{:S(2)}) %copy-start.4) | copy-done | bytes 65560
  6.9 0.8 %copy-done.5 = bf16[128,128]{1,0:T(8,128)(2,1)S(1)} copy-done((bf16[128,128]{1,0:T(8,128)(2,1)S(1)}, bf16[128,128]{1,0:T(8,128)(2,1)}, u32[]{:S(2)}) %copy-start.5) | copy-done | bytes 32792
  7.7 30.9 %shard_map.140 = (bf16[2,256]{1,0:T(2,128)(2,1)S(1)}, bf16[32,32,128]{2,1,0:T(8,128)(2,1)S(1)}) custom-call(f32[128,128]{1,0:T(8,128)S(1)} %copy-done.3, bf16[16,128]{1,0:T(8,128)(2,1)S(1)} %copy-done.6, f32[1,128]{1,0:T(1,128)S(1)} %bitcast.10, bf16[3,1152,128]{2,1,0:T(8,128)(2,1)S(1)} %bitcast.6, f32[3,1,128]{2,1,0:T(1,128)S(1)} %reshape.27.cb_ref, ...), custom_call_target="tpu_custom_call" | custom-call | tf_op jit(solution)/shard_map/pallas_call | solution.py:327
  38.6 0.6 %copy.17 = bf16[2,256]{1,0:T(2,128)(2,1)} copy(bf16[2,256]{1,0:T(2,128)(2,1)S(1)} %get-tuple-element.4) | data formatting | bytes 2048
  39.2 0.7 %copy.18 = bf16[32,32,128]{2,1,0:T(8,128)(2,1)} copy(bf16[32,32,128]{2,1,0:T(8,128)(2,1)S(1)} %get-tuple-element.5) | data formatting | bytes 524288
  (6 shorter events, 0.0 us)
Async XLA Ops:
  0.6 0.7 %copy-start.12 = (f32[3,128]{1,0:T(4,128)S(1)}, f32[3,128]{1,0:T(4,128)}, u32[]{:S(2)}) copy-start(f32[3,128]{1,0:T(4,128)} %param.17) | copy-start | bytes 4612
  0.6 0.7 %copy-start.9 = (f32[256]{0:T(256)S(1)}, f32[256]{0:T(256)}, u32[]{:S(2)}) copy-start(f32[256]{0:T(256)} %param.25) | copy-start | bytes 3076
  0.7 0.7 %copy-start.10 = (f32[128]{0:T(128)S(1)}, f32[128]{0:T(128)}, u32[]{:S(2)}) copy-start(f32[128]{0:T(128)} %param.15) | copy-start | bytes 1540
  0.7 0.7 %copy-start.11 = (f32[128]{0:T(128)S(1)}, f32[128]{0:T(128)}, u32[]{:S(2)}) copy-start(f32[128]{0:T(128)} %param.19) | copy-start | bytes 1540
  0.7 0.7 %copy-start.7 = (f32[1024]{0:T(1024)S(1)}, f32[1024]{0:T(1024)}, u32[]{:S(2)}) copy-start(f32[1024]{0:T(1024)} %param.23) | copy-start | bytes 12292
  0.7 0.7 %copy-start.6 = (bf16[16,128]{1,0:T(8,128)(2,1)S(1)}, bf16[16,128]{1,0:T(8,128)(2,1)}, u32[]{:S(2)}) copy-start(bf16[16,128]{1,0:T(8,128)(2,1)} %ew_ref.1) | copy-start | bytes 12292
  1.3 0.7 %copy-start.8 = (f32[256]{0:T(256)S(1)}, f32[256]{0:T(256)}, u32[]{:S(2)}) copy-start(f32[256]{0:T(256)} %param.21) | copy-start | bytes 3076
  2.0 1.2 %copy-start = (bf16[3,3,3,128,128]{4,3,2,1,0:T(8,128)(2,1)S(1)}, bf16[3,3,3,128,128]{4,3,2,1,0:T(8,128)(2,1)}, u32[]{:S(2)}) copy-start(bf16[3,3,3,128,128]{4,3,2,1,0:T(8,128)(2,1)} %param.16) | copy-start | bytes 2654212
  3.2 1.0 %copy-start.1 = (bf16[256,1024]{1,0:T(8,128)(2,1)S(1)}, bf16[256,1024]{1,0:T(8,128)(2,1)}, u32[]{:S(2)}) copy-start(bf16[256,1024]{1,0:T(8,128)(2,1)} %uw_hbm.1) | copy-start | bytes 1572868
  4.2 1.0 %copy-start.2 = (bf16[1024,256]{1,0:T(8,128)(2,1)S(1)}, bf16[1024,256]{1,0:T(8,128)(2,1)}, u32[]{:S(2)}) copy-start(bf16[1024,256]{1,0:T(8,128)(2,1)} %dw_hbm.1) | copy-start | bytes 1572868
  5.2 0.8 %copy-start.3 = (f32[128,128]{1,0:T(8,128)S(1)}, f32[128,128]{1,0:T(8,128)}, u32[]{:S(2)}) copy-start(f32[128,128]{1,0:T(8,128)} %x_ref.1) | copy-start | bytes 196612
  6.1 0.8 %copy-start.4 = (bf16[128,256]{1,0:T(8,128)(2,1)S(1)}, bf16[128,256]{1,0:T(8,128)(2,1)}, u32[]{:S(2)}) copy-start(bf16[128,256]{1,0:T(8,128)(2,1)} %pw_hbm.1) | copy-start | bytes 196612
  6.9 0.8 %copy-start.5 = (bf16[128,128]{1,0:T(8,128)(2,1)S(1)}, bf16[128,128]{1,0:T(8,128)(2,1)}, u32[]{:S(2)}) copy-start(bf16[128,128]{1,0:T(8,128)(2,1)} %mw_ref.1) | copy-start | bytes 98308

commit v2 on v1

--- a/solution.py
+++ b/solution.py
@@ -11,7 +11,7 @@
 LAYERS = 3
 TILE = 32
 BLK = 8
-PAD = 16
+PAD = 8
 SUB = 48
 CH = 128
 MESH = pl.DeviceIdType.MESH
@@ -44,21 +44,34 @@
 
 def kernel(
     n,
+    x_hbm,
+    ew_hbm,
+    eb_hbm,
+    cw_hbm,
+    cb_hbm,
+    mw_hbm,
+    mb_hbm,
+    pw_hbm,
+    pb_hbm,
+    uw_hbm,
+    ub_hbm,
+    dw_hbm,
+    db_hbm,
+    lat_hbm,
+    sym_hbm,
     x_ref,
     ew_ref,
     eb_ref,
-    cw_hbm,
+    cw,
     cb_ref,
     mw_ref,
     mb_ref,
-    pw_hbm,
+    pw,
     pb_ref,
-    uw_hbm,
+    uw,
     ub_ref,
-    dw_hbm,
+    dw,
     db_ref,
-    lat_ref,
-    sym_hbm,
     xt,
     own_p,
     own_q,
@@ -69,10 +82,7 @@
     f2,
     f3,
     symb,
-    cw,
-    pw,
-    uw,
-    dw,
+    lat_ref,
     part,
     got,
     near_ss,
@@ -88,12 +98,24 @@
     c = lax.axis_index("col")
     rows_each = TILE // n
 
-    weights = [
-        pltpu.make_async_copy(src, dst, wsem.at[k])
-        for k, (src, dst) in enumerate([(cw_hbm, cw), (pw_hbm, pw), (uw_hbm, uw), (dw_hbm, dw)])
+    held = [
+        (x_hbm, x_ref),
+        (ew_hbm, ew_ref),
+        (eb_hbm, eb_ref),
+        (cw_hbm, cw),
+        (cb_hbm, cb_ref),
+        (mw_hbm, mw_ref),
+        (mb_hbm, mb_ref),
+        (pw_hbm, pw),
+        (pb_hbm, pb_ref),
+        (uw_hbm, uw),
+        (ub_hbm, ub_ref),
+        (dw_hbm, dw),
+        (db_hbm, db_ref),
     ]
-    for w in weights:
-        w.start()
+    loads = [pltpu.make_async_copy(src, dst, wsem.at[k]) for k, (src, dst) in enumerate(held)]
+    for load in loads:
+        load.start()
 
     def inside(a, b):
         return (a >= 0) & (a < n) & (b >= 0) & (b < n)
@@ -116,6 +138,7 @@
     for k in range(1, n):
         greet(r, lax.rem(c + k, n))
 
+    loads[0].wait()
     xt[...] = x_ref[...].T
     y_p = jnp.concatenate([x_ref[pl.ds(s, TILE, stride=PATCH), :] for s in range(PATCH)], axis=1)
     y_q = jnp.concatenate([xt[pl.ds(s, TILE, stride=PATCH), :] for s in range(PATCH)], axis=1)
@@ -131,6 +154,8 @@
         own_q[h] = q_h
         near_h[h + 1, PAD : PAD + TILE, :] = q_h
 
+    for load in loads[1:]:
+        load.wait()
     pr = lax.broadcasted_iota(jnp.int32, (128, 16), 0)
     pc = lax.broadcasted_iota(jnp.int32, (128, 16), 1)
     rid = lax.broadcasted_iota(jnp.int32, (128, 128), 0) >> 4
@@ -208,7 +233,7 @@
             wide = jnp.dot(patches[h], diag, preferred_element_type=F32)
             cells = jnp.concatenate(
                 [
-                    (wide[8:56, b * CH : (b + 1) * CH] + eb_ref[...])[None]
+                    (wide[:, b * CH : (b + 1) * CH] + eb_ref[...])[None]
                     for b in range(first, last)
                 ],
                 axis=0,
@@ -225,7 +250,7 @@
                 pieces.append(piece.reshape(count_l * piece.shape[1], CH))
         lhs = jnp.concatenate(pieces, axis=1)
         total = jnp.dot(lhs, cw[layer], preferred_element_type=F32)
-        return gelu(total + cb_ref[layer])
+        return gelu(total + cb_ref[layer : layer + 1])
 
     def features(lead_is_row, finish):
         for at in range(0, 36, 12):
@@ -241,7 +266,6 @@
     for ok, got_in in near_in:
         pl.when(ok)(got_in.wait_recv)
     embed(near_h, diag_q)
-    weights[0].wait()
 
     def keep_own(at, value):
         f3[at * TILE : (at + 16) * TILE, :] = value
@@ -259,7 +283,9 @@
         mean = (f3[at * TILE : (at + 16) * TILE, :].astype(F32) + value.astype(F32)) * 0.5
         sym = mean.astype(BF16)
         symb[at : at + 16] = sym.reshape(16, TILE, CH)
-        out = pltpu.make_async_copy(symb.at[pl.ds(at, 16)], sym_hbm.at[pl.ds(at, 16)], osem.at[at // 16])
+        out = pltpu.make_async_copy(
+            symb.at[pl.ds(at, 16)], sym_hbm.at[pl.ds(at, 16)], osem.at[at // 16]
+        )
         out.start()
         outs.append(out)
         mixed = gelu(jnp.dot(sym, mw_ref[...], preferred_element_type=F32) + mb_ref[...])
@@ -282,8 +308,6 @@
         )
         move.start()
         moves.append(move)
-    for w in weights[1:]:
-        w.wait()
     for move in moves:
         move.wait_recv()
     summed = part[c]
@@ -294,6 +318,9 @@
     hidden = gelu(jnp.dot(latent.astype(BF16), uw[...], preferred_element_type=F32) + ub_ref[...])
     result = latent + jnp.dot(hidden.astype(BF16), dw[...], preferred_element_type=F32) + db_ref[...]
     lat_ref[...] = result.astype(BF16)
+    out = pltpu.make_async_copy(lat_ref, lat_hbm, osem.at[2])
+    out.start()
+    outs.append(out)
 
     for move in moves:
         move.wait_send()
@@ -301,6 +328,26 @@
         pl.when(ok)(out.wait_send)
     for out in outs:
         out.wait()
+
+
+def hand_over(lat_ref, sym_ref, lat_out, sym_out, lat_held, sym_held, sem_in, sem_out):
+    steps = [(lat_ref, lat_held, lat_out)]
+    for k in range(0, TILE, TILE // 4):
+        part = pl.ds(k, TILE // 4)
+        steps.append((sym_ref.at[part], sym_held.at[part], sym_out.at[part]))
+    takes = [
+        pltpu.make_async_copy(src, mid, sem_in.at[k]) for k, (src, mid, _) in enumerate(steps)
+    ]
+    gives = [
+        pltpu.make_async_copy(mid, dst, sem_out.at[k]) for k, (_, mid, dst) in enumerate(steps)
+    ]
+    for take in takes:
+        take.start()
+    for take, give in zip(takes, gives):
+        take.wait()
+        give.start()
+    for give in gives:
+        give.wait()
 
 
 def body(
@@ -322,17 +369,34 @@
     rows_each = TILE // n
     latent_width, hidden_width = up_weight.shape
     vmem = pl.BlockSpec(memory_space=pltpu.VMEM)
-    hbm = pl.BlockSpec(memory_space=pl.ANY)
+    hbm = pl.BlockSpec(memory_space=pltpu.HBM)
     dma = pltpu.SemaphoreType.DMA
-    return pl.pallas_call(
+    args = (
+        contact_map,
+        embed_weight,
+        embed_bias.reshape(1, CH),
+        conv_weight.reshape(LAYERS, 9 * CH, CH),
+        conv_bias,
+        mix_weight,
+        mix_bias.reshape(1, CH),
+        proj_weight,
+        proj_bias.reshape(1, latent_width),
+        up_weight,
+        up_bias.reshape(1, hidden_width),
+        down_weight,
+        down_bias.reshape(1, latent_width),
+    )
+    shapes = (
+        jax.ShapeDtypeStruct((rows_each, latent_width), BF16),
+        jax.ShapeDtypeStruct((TILE, TILE, CH), BF16),
+    )
+    done = pl.pallas_call(
         functools.partial(kernel, n),
-        out_shape=(
-            jax.ShapeDtypeStruct((rows_each, latent_width), BF16),
-            jax.ShapeDtypeStruct((TILE, TILE, CH), BF16),
-        ),
-        in_specs=[vmem, vmem, vmem, hbm, vmem, vmem, vmem, hbm, vmem, hbm, vmem, hbm, vmem],
-        out_specs=(vmem, hbm),
-        scratch_shapes=[
+        out_shape=shapes,
+        in_specs=[hbm] * len(args),
+        out_specs=(hbm, hbm),
+        scratch_shapes=[pltpu.VMEM(a.shape, a.dtype) for a in args]
+        + [
             pltpu.VMEM((TILE * PATCH, TILE * PATCH), F32),
             pltpu.VMEM((4, TILE, 128), BF16),
             pltpu.VMEM((4, TILE, 128), BF16),
@@ -342,11 +406,8 @@
             pltpu.VMEM((3, 36, SUB, CH), BF16),
             pltpu.VMEM((3, 34, TILE, CH), BF16),
             pltpu.VMEM((TILE * TILE, CH), BF16),
-            pltpu.VMEM((TILE, TILE, CH), BF16),
-            pltpu.VMEM((LAYERS, 9 * CH, CH), BF16),
-            pltpu.VMEM(proj_weight.shape, BF16),
-            pltpu.VMEM(up_weight.shape, BF16),
-            pltpu.VMEM(down_weight.shape, BF16),
+            pltpu.VMEM(shapes[1].shape, BF16),
+            pltpu.VMEM(shapes[0].shape, BF16),
             pltpu.VMEM((n, rows_each, CH), F32),
             pltpu.VMEM((n, rows_each, CH), F32),
             dma((9,)),
@@ -355,27 +416,21 @@
             dma((9,)),
             dma((n,)),
             dma((n,)),
-            dma((4,)),
-            dma((2,)),
+            dma((len(args),)),
+            dma((3,)),
         ],
         compiler_params=pltpu.CompilerParams(
-            collective_id=0, has_side_effects=True, vmem_limit_bytes=48 * 1024 * 1024
+            collective_id=0, has_side_effects=True, vmem_limit_bytes=67043328
         ),
-    )(
-        contact_map,
-        embed_weight,
-        embed_bias.reshape(1, CH),
-        conv_weight.reshape(LAYERS, 9 * CH, CH),
-        conv_bias.reshape(LAYERS, 1, CH),
-        mix_weight,
-        mix_bias.reshape(1, CH),
-        proj_weight,
-        proj_bias.reshape(1, latent_width),
-        up_weight,
-        up_bias.reshape(1, hidden_width),
-        down_weight,
-        down_bias.reshape(1, latent_width),
-    )
+    )(*args)
+    return pl.pallas_call(
+        hand_over,
+        out_shape=shapes,
+        in_specs=[hbm, hbm],
+        out_specs=(hbm, hbm),
+        scratch_shapes=[pltpu.VMEM(shape.shape, BF16) for shape in shapes]
+        + [dma((5,)), dma((5,))],
+    )(*done)
 
 
 def solution(mesh):

time: 40.3 us -> 32 us (0.79)
  local copies, waits for them, and re-layouts: 8.26 us -> 0 us
    unnamed x28 -> x0, local copies, waits for them, and re-layouts: 8.26 us -> none
    pallas_call x1 -> x2, Pallas kernels: 30.9 us -> 31.2 us  [the longest x1 29.5 us: body(): pl.pallas_call(functools.partial(kernel, n), out_shape=shapes, in_specs=[...]
where the time goes in v2:
time: 32 us; the launch traced here: 31.8 us
  Pallas kernels  31.2 us (98%)
  between operations  0.64 us (2%)
    pallas_call x1, Pallas kernels, body(): pl.pallas_call(functools.partial(kernel, n), out_shape=shapes, in_specs=[...  29.5 us
    pallas_call x1, Pallas kernels, body(): pl.pallas_call(hand_over, out_shape=shapes, in_specs=[hbm, hbm], out_spec...  1.65 us

profile of v2, /device:TPU:1, one launch (start us, length us, event | category | flops | bytes accessed | tf_op | source)
XLA Modules:
  0.0 31.8 jit_solution(4760871166913774465)
XLA Ops:
  0.6 29.5 %shard_map.140 = (bf16[2,256]{1,0:T(2,128)(2,1)}, bf16[32,32,128]{2,1,0:T(8,128)(2,1)}) custom-call(f32[128,128]{1,0:T(8,128)} %x_hbm.1, bf16[16,128]{1,0:T(8,128)(2,1)} %ew_hbm.1, f32[1,128]{1,0:T(1,128)} %bitcast.10, bf16[3,1152,128]{2,1,0:T(8,128)(2,1)} %bitcast.6, f32[3,128]{1,0:T(4,128)} %cb_hbm.1, bf16[128,128]{1,0:T(8,128)(2,1)} %mw_hbm.1, ...), custom_call_target="tpu_custom_call" | custom-call | tf_op jit(solution)/shard_map/pallas_call | solution.py:393
  30.2 1.7 %shard_map.141 = (bf16[2,256]{1,0:T(2,128)(2,1)}, bf16[32,32,128]{2,1,0:T(8,128)(2,1)}) custom-call(bf16[2,256]{1,0:T(2,128)(2,1)} %get-tuple-element.4.lat_ref, bf16[32,32,128]{2,1,0:T(8,128)(2,1)} %get-tuple-element.5.sym_ref), custom_call_target="tpu_custom_call" | custom-call | tf_op jit(solution)/shard_map/pallas_call | solution.py:426

commit v3 on v2

--- a/solution.py
+++ b/solution.py
@@ -17,6 +17,7 @@
 MESH = pl.DeviceIdType.MESH
 F32 = jnp.float32
 BF16 = jnp.bfloat16
+CUTS = [[(0, 9), (9, 9)], [(0, 9), (9, 8)], [(0, 8), (8, 8)]]
 OFFSETS = [(dl, ds) for dl in (-1, 0, 1) for ds in (-1, 0, 1)]
 
 
@@ -81,6 +82,7 @@
     f1,
     f2,
     f3,
+    acc,
     symb,
     lat_ref,
     part,
@@ -113,10 +115,6 @@
         (dw_hbm, dw),
         (db_hbm, db_ref),
     ]
-    loads = [pltpu.make_async_copy(src, dst, wsem.at[k]) for k, (src, dst) in enumerate(held)]
-    for load in loads:
-        load.start()
-
     def inside(a, b):
         return (a >= 0) & (a < n) & (b >= 0) & (b < n)
 
@@ -138,6 +136,9 @@
     for k in range(1, n):
         greet(r, lax.rem(c + k, n))
 
+    loads = [pltpu.make_async_copy(src, dst, wsem.at[k]) for k, (src, dst) in enumerate(held)]
+    for load in loads:
+        load.start()
     loads[0].wait()
     xt[...] = x_ref[...].T
     y_p = jnp.concatenate([x_ref[pl.ds(s, TILE, stride=PATCH), :] for s in range(PATCH)], axis=1)
@@ -213,11 +214,11 @@
 
     def masked(value, first):
         count_l = value.shape[0]
-        lead = r * TILE + first + lax.broadcasted_iota(jnp.int32, (count_l, SUB, 1), 0)
+        lead = r * TILE + first + 2 * lax.broadcasted_iota(jnp.int32, (count_l, SUB, 1), 0)
         ok = sub_ok & (lead >= 0) & (lead < n * TILE)
         return jnp.where(ok, value, 0.0)
 
-    def put(ref, at, value, cut=False):
+    def put(ref, parity, at, value, cut=False):
         count_l = value.shape[0]
         flat = value.reshape(count_l * SUB, CH)
         for s in range(3):
@@ -225,50 +226,68 @@
             moved = moved.reshape(count_l, SUB, CH)
             if cut:
                 moved = moved[:, 8:40, :]
-            ref[s, at : at + count_l] = moved.astype(BF16)
+            ref[s, parity, at : at + count_l] = moved.astype(BF16)
 
     def embed(patches, diag):
         for h in range(6):
             first, last = (5, 8) if h == 0 else (0, 3) if h == 5 else (0, 8)
             wide = jnp.dot(patches[h], diag, preferred_element_type=F32)
-            cells = jnp.concatenate(
-                [
-                    (wide[:, b * CH : (b + 1) * CH] + eb_ref[...])[None]
-                    for b in range(first, last)
-                ],
-                axis=0,
-            )
-            at = h * BLK + first - 5
-            put(f0, at, masked(cells, at - 3))
-
-    def conv(layer, src, at, count_l, lead_is_row):
-        pieces = []
-        for a in range(3):
-            for b in range(3):
-                lead, sub = (a, b) if lead_is_row else (b, a)
-                piece = src[sub, at + lead : at + lead + count_l]
-                pieces.append(piece.reshape(count_l * piece.shape[1], CH))
+            for start in (first, first + 1):
+                cells = jnp.concatenate(
+                    [
+                        (wide[:, b * CH : (b + 1) * CH] + eb_ref[...])[None]
+                        for b in range(start, last, 2)
+                    ],
+                    axis=0,
+                )
+                at = h * BLK + start - 5
+                put(f0, at % 2, at // 2, masked(cells, at - 3))
+
+    def conv(layer, src, at, pairs, lead_is_row, slot):
+        def tap(lead, sub):
+            if lead < 0 or lead > 2:
+                return jnp.zeros((CH, CH), BF16)
+            k = lead * 3 + sub if lead_is_row else sub * 3 + lead
+            return cw[layer, k * CH : (k + 1) * CH, :]
+
+        pieces, taps = [], []
+        for lead in range(4):
+            for sub in range(3):
+                first = at + lead // 2
+                piece = src[sub, lead % 2, first : first + pairs]
+                pieces.append(piece.reshape(pairs * piece.shape[1], CH))
+                taps.append(jnp.concatenate([tap(lead, sub), tap(lead - 1, sub)], axis=1))
         lhs = jnp.concatenate(pieces, axis=1)
-        total = jnp.dot(lhs, cw[layer], preferred_element_type=F32)
+        rows = pairs * SUB if layer < 2 else pairs * TILE
+        acc[slot, :rows] = jnp.dot(lhs, jnp.concatenate(taps, axis=0), preferred_element_type=F32)
+
+    def cell_row(layer, slot, k, h):
+        each = SUB if layer < 2 else TILE
+        total = acc[slot, k * each : (k + 1) * each, h * CH : (h + 1) * CH]
         return gelu(total + cb_ref[layer : layer + 1])
 
     def features(lead_is_row, finish):
-        for at in range(0, 36, 12):
-            v = conv(0, f0, at, 12, lead_is_row).reshape(12, SUB, CH)
-            put(f1, at, masked(v, at - 2))
-        for at in range(0, 34, 17):
-            v = conv(1, f1, at, 17, lead_is_row).reshape(17, SUB, CH)
-            put(f2, at, masked(v, at - 1), cut=True)
-        for at in range(0, TILE, 16):
-            finish(at, conv(2, f2, at, 16, lead_is_row).astype(BF16))
+        slot = 0
+        for layer, (src, dst) in enumerate([(f0, f1), (f1, f2), (f2, None)]):
+            for at, pairs in CUTS[layer]:
+                conv(layer, src, at, pairs, lead_is_row, slot)
+                for k in range(pairs):
+                    for h in (0, 1):
+                        v = cell_row(layer, slot, k, h)
+                        if dst is None:
+                            finish(at + k, h, v.astype(BF16))
+                        else:
+                            lead = 2 * (at + k) + h - 2 + layer
+                            put(dst, h, at + k, masked(v[None], lead), cut=layer == 1)
+                slot = 1 - slot
 
     diag_q = block_diagonal(True)
     for ok, got_in in near_in:
         pl.when(ok)(got_in.wait_recv)
     embed(near_h, diag_q)
 
-    def keep_own(at, value):
-        f3[at * TILE : (at + 16) * TILE, :] = value
+    def keep_own(m, h, value):
+        f3[2 * m + h] = value
 
     features(True, keep_own)
 
@@ -279,21 +298,23 @@
 
     outs = []
 
-    def finish_far(at, value):
-        mean = (f3[at * TILE : (at + 16) * TILE, :].astype(F32) + value.astype(F32)) * 0.5
-        sym = mean.astype(BF16)
-        symb[at : at + 16] = sym.reshape(16, TILE, CH)
-        out = pltpu.make_async_copy(
-            symb.at[pl.ds(at, 16)], sym_hbm.at[pl.ds(at, 16)], osem.at[at // 16]
-        )
+    def finish_far(m, h, value):
+        i = 2 * m + h
+        symb[i] = ((f3[i].astype(F32) + value.astype(F32)) * 0.5).astype(BF16)
+
+    features(False, finish_far)
+    for at in range(0, TILE, 8):
+        rows = pl.ds(at, 8)
+        out = pltpu.make_async_copy(symb.at[rows], sym_hbm.at[rows], osem.at[at // 8])
         out.start()
         outs.append(out)
-        mixed = gelu(jnp.dot(sym, mw_ref[...], preferred_element_type=F32) + mb_ref[...])
-        sums = jnp.sum(mixed.reshape(16, TILE, CH), axis=1)
-        for g in range(16 // rows_each):
-            part[at // rows_each + g] = sums[g * rows_each : (g + 1) * rows_each]
-
-    features(False, finish_far)
+        mixed = jnp.dot(
+            symb[rows].reshape(8 * TILE, CH), mw_ref[...], preferred_element_type=F32
+        )
+        sums = jnp.sum(gelu(mixed + mb_ref[...]).reshape(8, TILE, CH), axis=1)
+        for k in range(8):
+            row = at + k
+            part[row // rows_each, row % rows_each : row % rows_each + 1] = sums[k : k + 1]
 
     moves = []
     for k in range(1, n):
@@ -318,7 +339,7 @@
     hidden = gelu(jnp.dot(latent.astype(BF16), uw[...], preferred_element_type=F32) + ub_ref[...])
     result = latent + jnp.dot(hidden.astype(BF16), dw[...], preferred_element_type=F32) + db_ref[...]
     lat_ref[...] = result.astype(BF16)
-    out = pltpu.make_async_copy(lat_ref, lat_hbm, osem.at[2])
+    out = pltpu.make_async_copy(lat_ref, lat_hbm, osem.at[len(outs)])
     out.start()
     outs.append(out)
 
@@ -402,10 +423,11 @@
             pltpu.VMEM((4, TILE, 128), BF16),
             pltpu.VMEM((6, TILE + 2 * PAD, 128), BF16),
             pltpu.VMEM((6, TILE + 2 * PAD, 128), BF16),
-            pltpu.VMEM((3, 38, SUB, CH), BF16),
-            pltpu.VMEM((3, 36, SUB, CH), BF16),
-            pltpu.VMEM((3, 34, TILE, CH), BF16),
-            pltpu.VMEM((TILE * TILE, CH), BF16),
+            pltpu.VMEM((3, 2, 19, SUB, CH), BF16),
+            pltpu.VMEM((3, 2, 18, SUB, CH), BF16),
+            pltpu.VMEM((3, 2, 17, TILE, CH), BF16),
+            pltpu.VMEM((TILE, TILE, CH), BF16),
+            pltpu.VMEM((2, 9 * SUB, 2 * CH), F32),
             pltpu.VMEM(shapes[1].shape, BF16),
             pltpu.VMEM(shapes[0].shape, BF16),
             pltpu.VMEM((n, rows_each, CH), F32),
@@ -417,7 +439,7 @@
             dma((n,)),
             dma((n,)),
             dma((len(args),)),
-            dma((3,)),
+            dma((5,)),
         ],
         compiler_params=pltpu.CompilerParams(
             collective_id=0, has_side_effects=True, vmem_limit_bytes=67043328

time: 32 us -> 30.7 us (0.959)
  Pallas kernels: 31.2 us -> 29.9 us
    pallas_call x1, Pallas kernels: 29.5 us -> 28.2 us  [body(): pl.pallas_call(functools.partial(kernel, n), out_shape=shapes, in_specs=[...]
where the time goes in v3:
time: 30.7 us; the launch traced here: 30.5 us
  Pallas kernels  29.9 us (97%)
  between operations  0.64 us (2%)
    pallas_call x1, Pallas kernels, body(): pl.pallas_call(functools.partial(kernel, n), out_shape=shapes, in_specs=[...  28.2 us
    pallas_call x1, Pallas kernels, body(): pl.pallas_call(hand_over, out_shape=shapes, in_specs=[hbm, hbm], out_spec...  1.65 us

profile of v3, /device:TPU:1, one launch (start us, length us, event | category | flops | bytes accessed | tf_op | source)
XLA Modules:
  0.0 30.5 jit_solution(6776304520884061306)
XLA Ops:
  0.6 28.2 %shard_map.140 = (bf16[2,256]{1,0:T(2,128)(2,1)}, bf16[32,32,128]{2,1,0:T(8,128)(2,1)}) custom-call(f32[128,128]{1,0:T(8,128)} %x_hbm.1, bf16[16,128]{1,0:T(8,128)(2,1)} %ew_hbm.1, f32[1,128]{1,0:T(1,128)} %bitcast.10, bf16[3,1152,128]{2,1,0:T(8,128)(2,1)} %bitcast.6, f32[3,128]{1,0:T(4,128)} %cb_hbm.1, bf16[128,128]{1,0:T(8,128)(2,1)} %mw_hbm.1, ...), custom_call_target="tpu_custom_call" | custom-call | tf_op jit(solution)/shard_map/pallas_call | solution.py:414
  28.9 1.7 %shard_map.141 = (bf16[2,256]{1,0:T(2,128)(2,1)}, bf16[32,32,128]{2,1,0:T(8,128)(2,1)}) custom-call(bf16[2,256]{1,0:T(2,128)(2,1)} %get-tuple-element.4.lat_ref, bf16[32,32,128]{2,1,0:T(8,128)(2,1)} %get-tuple-element.5.sym_ref), custom_call_target="tpu_custom_call" | custom-call | tf_op jit(solution)/shard_map/pallas_call | solution.py:448

commit v4 on v3

--- a/solution.py
+++ b/solution.py
@@ -17,14 +17,17 @@
 MESH = pl.DeviceIdType.MESH
 F32 = jnp.float32
 BF16 = jnp.bfloat16
-CUTS = [[(0, 9), (9, 9)], [(0, 9), (9, 8)], [(0, 8), (8, 8)]]
+CUTS = [[(0, 6), (6, 6), (12, 6)], [(0, 6), (6, 6), (12, 5)], [(0, 6), (6, 5), (11, 5)]]
 OFFSETS = [(dl, ds) for dl in (-1, 0, 1) for ds in (-1, 0, 1)]
 
 
+def gelu_of_half(half):
+    inner = half * (2 * 0.7978845608028654 + (8 * 0.7978845608028654 * 0.044715) * (half * half))
+    return half + half * jnp.tanh(inner)
+
+
 def gelu(x):
-    half = 0.5 * x
-    inner = x * (0.7978845608028654 + (0.7978845608028654 * 0.044715) * (x * x))
-    return half + half * jnp.tanh(inner)
+    return gelu_of_half(0.5 * x)
 
 
 def lead_src(d):
@@ -83,6 +86,7 @@
     f2,
     f3,
     acc,
+    stage,
     symb,
     lat_ref,
     part,
@@ -155,8 +159,6 @@
         own_q[h] = q_h
         near_h[h + 1, PAD : PAD + TILE, :] = q_h
 
-    for load in loads[1:]:
-        load.wait()
     pr = lax.broadcasted_iota(jnp.int32, (128, 16), 0)
     pc = lax.broadcasted_iota(jnp.int32, (128, 16), 1)
     rid = lax.broadcasted_iota(jnp.int32, (128, 128), 0) >> 4
@@ -202,6 +204,16 @@
                 (inside(r + dl, c + ds), message(own_q, near_h, near_ss, near_rs, dl, ds, r, c))
             )
 
+    for load in loads[1:]:
+        load.wait()
+    for layer in range(LAYERS):
+        for k in range(9):
+            tap_rows = pl.ds(k * CH, CH)
+            cw[layer, tap_rows, :] = cw[layer, tap_rows, :] * jnp.bfloat16(0.5)
+    mw_ref[...] = mw_ref[...] * jnp.bfloat16(0.5)
+    cb_half = cb_ref[...] * 0.5
+    mb_half = mb_ref[...] * 0.5
+
     def keep(dl, ds):
         far_h[lead_dst(dl), sub_dst(ds), :] = own_p[lead_src(dl), sub_src(ds), :]
 
@@ -209,39 +221,36 @@
     pl.when(c == r + 1)(functools.partial(keep, 1, -1))
     pl.when(c == r - 1)(functools.partial(keep, -1, 1))
 
-    sub_cell = c * TILE - 8 + lax.broadcasted_iota(jnp.int32, (1, SUB, 1), 1)
+    sub_cell = c * TILE - 8 + lax.broadcasted_iota(jnp.int32, (SUB, 1), 0)
     sub_ok = (sub_cell >= 0) & (sub_cell < n * TILE)
 
+    keep_sub = jnp.broadcast_to(sub_ok.astype(F32), (SUB, CH))
+
+    def lead_ok(first):
+        lead = r * TILE + first
+        return (lead >= 0) & (lead < n * TILE)
+
     def masked(value, first):
-        count_l = value.shape[0]
-        lead = r * TILE + first + 2 * lax.broadcasted_iota(jnp.int32, (count_l, SUB, 1), 0)
-        ok = sub_ok & (lead >= 0) & (lead < n * TILE)
-        return jnp.where(ok, value, 0.0)
+        keep = keep_sub
+        if first < 0 or first >= TILE:
+            keep = keep * lead_ok(first).astype(F32)
+        return value * keep
 
     def put(ref, parity, at, value, cut=False):
-        count_l = value.shape[0]
-        flat = value.reshape(count_l * SUB, CH)
+        line = stage.at[parity, at]
+        line[8 : 8 + SUB, :] = value
+        first, rows = (16, TILE) if cut else (8, SUB)
         for s in range(3):
-            moved = flat if s == 1 else pltpu.roll(flat, 1 if s == 0 else count_l * SUB - 1, 0)
-            moved = moved.reshape(count_l, SUB, CH)
-            if cut:
-                moved = moved[:, 8:40, :]
-            ref[s, parity, at : at + count_l] = moved.astype(BF16)
+            ref[s, parity, at] = line[pl.ds(first + s - 1, rows), :].astype(BF16)
 
     def embed(patches, diag):
         for h in range(6):
             first, last = (5, 8) if h == 0 else (0, 3) if h == 5 else (0, 8)
             wide = jnp.dot(patches[h], diag, preferred_element_type=F32)
-            for start in (first, first + 1):
-                cells = jnp.concatenate(
-                    [
-                        (wide[:, b * CH : (b + 1) * CH] + eb_ref[...])[None]
-                        for b in range(start, last, 2)
-                    ],
-                    axis=0,
-                )
-                at = h * BLK + start - 5
-                put(f0, at % 2, at // 2, masked(cells, at - 3))
+            for b in range(first, last):
+                at = h * BLK + b - 5
+                cells = wide[:, b * CH : (b + 1) * CH] + eb_ref[...]
+                put(f0, at % 2, at // 2, jnp.where(sub_ok & lead_ok(at - 3), cells, 0.0))
 
     def conv(layer, src, at, pairs, lead_is_row, slot):
         def tap(lead, sub):
@@ -264,22 +273,30 @@
     def cell_row(layer, slot, k, h):
         each = SUB if layer < 2 else TILE
         total = acc[slot, k * each : (k + 1) * each, h * CH : (h + 1) * CH]
-        return gelu(total + cb_ref[layer : layer + 1])
-
-    def features(lead_is_row, finish):
-        slot = 0
-        for layer, (src, dst) in enumerate([(f0, f1), (f1, f2), (f2, None)]):
-            for at, pairs in CUTS[layer]:
-                conv(layer, src, at, pairs, lead_is_row, slot)
-                for k in range(pairs):
-                    for h in (0, 1):
-                        v = cell_row(layer, slot, k, h)
-                        if dst is None:
-                            finish(at + k, h, v.astype(BF16))
-                        else:
-                            lead = 2 * (at + k) + h - 2 + layer
-                            put(dst, h, at + k, masked(v[None], lead), cut=layer == 1)
-                slot = 1 - slot
+        return gelu_of_half(total + cb_half[layer : layer + 1])
+
+    def features(lead_is_row, finish, finish_block):
+        maps = [(f0, f1), (f1, f2), (f2, None)]
+        tasks = [(layer, at, pairs) for layer in range(LAYERS) for at, pairs in CUTS[layer]]
+
+        def multiply(t):
+            layer, at, pairs = tasks[t]
+            conv(layer, maps[layer][0], at, pairs, lead_is_row, t % 2)
+
+        multiply(0)
+        for t, (layer, at, pairs) in enumerate(tasks):
+            if t + 1 < len(tasks):
+                multiply(t + 1)
+            for k in range(pairs):
+                for h in (0, 1):
+                    v = cell_row(layer, t % 2, k, h)
+                    if layer == LAYERS - 1:
+                        finish(at + k, h, v.astype(BF16))
+                    else:
+                        lead = 2 * (at + k) + h - 2 + layer
+                        put(maps[layer][1], h, at + k, masked(v, lead), cut=layer == 1)
+            if layer == LAYERS - 1:
+                finish_block(2 * at, 2 * pairs)
 
     diag_q = block_diagonal(True)
     for ok, got_in in near_in:
@@ -289,7 +306,7 @@
     def keep_own(m, h, value):
         f3[2 * m + h] = value
 
-    features(True, keep_own)
+    features(True, keep_own, lambda first, count_l: None)
 
     diag_p = block_diagonal(False)
     for ok, got_in in far_in:
@@ -302,19 +319,20 @@
         i = 2 * m + h
         symb[i] = ((f3[i].astype(F32) + value.astype(F32)) * 0.5).astype(BF16)
 
-    features(False, finish_far)
-    for at in range(0, TILE, 8):
-        rows = pl.ds(at, 8)
-        out = pltpu.make_async_copy(symb.at[rows], sym_hbm.at[rows], osem.at[at // 8])
+    def mix_block(first, count_l):
+        rows = pl.ds(first, count_l)
+        out = pltpu.make_async_copy(symb.at[rows], sym_hbm.at[rows], osem.at[len(outs)])
         out.start()
         outs.append(out)
         mixed = jnp.dot(
-            symb[rows].reshape(8 * TILE, CH), mw_ref[...], preferred_element_type=F32
+            symb[rows].reshape(count_l * TILE, CH), mw_ref[...], preferred_element_type=F32
         )
-        sums = jnp.sum(gelu(mixed + mb_ref[...]).reshape(8, TILE, CH), axis=1)
-        for k in range(8):
-            row = at + k
+        sums = jnp.sum(gelu_of_half(mixed + mb_half).reshape(count_l, TILE, CH), axis=1)
+        for k in range(count_l):
+            row = first + k
             part[row // rows_each, row % rows_each : row % rows_each + 1] = sums[k : k + 1]
+
+    features(False, finish_far, mix_block)
 
     moves = []
     for k in range(1, n):
@@ -427,7 +445,8 @@
             pltpu.VMEM((3, 2, 18, SUB, CH), BF16),
             pltpu.VMEM((3, 2, 17, TILE, CH), BF16),
             pltpu.VMEM((TILE, TILE, CH), BF16),
-            pltpu.VMEM((2, 9 * SUB, 2 * CH), F32),
+            pltpu.VMEM((2, 6 * SUB, 2 * CH), F32),
+            pltpu.VMEM((2, 19, SUB + 16, CH), F32),
             pltpu.VMEM(shapes[1].shape, BF16),
             pltpu.VMEM(shapes[0].shape, BF16),
             pltpu.VMEM((n, rows_each, CH), F32),

time: 30.7 us -> 30 us (0.977)
  Pallas kernels: 29.9 us -> 29.2 us
    pallas_call x1, Pallas kernels: 28.2 us -> 27.5 us  [body(): pl.pallas_call(functools.partial(kernel, n), out_shape=shapes, in_specs=[...]
where the time goes in v4:
time: 30 us; the launch traced here: 29.8 us
  Pallas kernels  29.2 us (97%)
  between operations  0.64 us (2%)
    pallas_call x1, Pallas kernels, body(): pl.pallas_call(functools.partial(kernel, n), out_shape=shapes, in_specs=[...  27.5 us
    pallas_call x1, Pallas kernels, body(): pl.pallas_call(hand_over, out_shape=shapes, in_specs=[hbm, hbm], out_spec...  1.65 us

profile of v4, /device:TPU:1, one launch (start us, length us, event | category | flops | bytes accessed | tf_op | source)
XLA Modules:
  0.0 29.8 jit_solution(10505090100288465285)
XLA Ops:
  0.6 27.5 %shard_map.140 = (bf16[2,256]{1,0:T(2,128)(2,1)}, bf16[32,32,128]{2,1,0:T(8,128)(2,1)}) custom-call(f32[128,128]{1,0:T(8,128)} %x_hbm.1, bf16[16,128]{1,0:T(8,128)(2,1)} %ew_hbm.1, f32[1,128]{1,0:T(1,128)} %bitcast.10, bf16[3,1152,128]{2,1,0:T(8,128)(2,1)} %bitcast.6, f32[3,128]{1,0:T(4,128)} %cb_hbm.1, bf16[128,128]{1,0:T(8,128)(2,1)} %mw_hbm.1, ...), custom_call_target="tpu_custom_call" | custom-call | tf_op jit(solution)/shard_map/pallas_call | solution.py:432
  28.2 1.7 %shard_map.141 = (bf16[2,256]{1,0:T(2,128)(2,1)}, bf16[32,32,128]{2,1,0:T(8,128)(2,1)}) custom-call(bf16[2,256]{1,0:T(2,128)(2,1)} %get-tuple-element.4.lat_ref, bf16[32,32,128]{2,1,0:T(8,128)(2,1)} %get-tuple-element.5.sym_ref), custom_call_target="tpu_custom_call" | custom-call | tf_op jit(solution)/shard_map/pallas_call | solution.py:467

commit v5 on v4

--- a/solution.py
+++ b/solution.py
@@ -81,6 +81,12 @@
     own_q,
     near_h,
     far_h,
+    side_p,
+    side_q,
+    near_side,
+    far_side,
+    pack,
+    line_buf,
     f0,
     f1,
     f2,
@@ -151,13 +157,21 @@
     k = lax.broadcasted_iota(jnp.int32, (512, 512), 0)
     target = ((k >> 5) & 3) * 128 + ((k >> 2) & 7) * 16 + (k >> 7) * 4 + (k & 3)
     perm = (lax.broadcasted_iota(jnp.int32, (512, 512), 1) == target).astype(F32).astype(BF16)
-    z = jnp.dot(y, perm, preferred_element_type=F32).astype(BF16)
-    for h in range(4):
-        p_h = z[:TILE, h * 128 : (h + 1) * 128]
-        q_h = z[TILE:, h * 128 : (h + 1) * 128]
-        own_p[h] = p_h
-        own_q[h] = q_h
-        near_h[h + 1, PAD : PAD + TILE, :] = q_h
+    z = jnp.dot(y, perm, preferred_element_type=F32)
+    left = lax.broadcasted_iota(jnp.int32, (16, 128), 1) < 64
+    for m, (own, side) in enumerate([(own_p, side_p), (own_q, side_q)]):
+        slabs = [z[m * TILE : (m + 1) * TILE, h * 128 : (h + 1) * 128] for h in range(4)]
+        for h in range(4):
+            own[h] = slabs[h].astype(BF16)
+            if m == 1:
+                near_h[h + 1, PAD : PAD + TILE, :] = slabs[h].astype(BF16)
+            pack[2 * m, 4 * h : 4 * h + 4, :] = slabs[h][TILE - 4 :, :]
+            pack[2 * m + 1, 4 * h : 4 * h + 4, :] = slabs[h][:4, :]
+        side[0] = pack[2 * m].astype(BF16)
+        side[1] = pack[2 * m + 1].astype(BF16)
+        end, start = slabs[3], slabs[0]
+        side[2] = jnp.where(left, pltpu.roll(end[:16], 64, 1), end[16:]).astype(BF16)
+        side[3] = jnp.where(left, start[:16], pltpu.roll(start[16:], 64, 1)).astype(BF16)
 
     pr = lax.broadcasted_iota(jnp.int32, (128, 16), 0)
     pc = lax.broadcasted_iota(jnp.int32, (128, 16), 1)
@@ -175,9 +189,15 @@
 
     def message(src, dst, ss, rs, dl, ds, a, b):
         i = (dl + 1) * 3 + ds + 1
+        if (dl == 0) != (ds == 0):
+            k = (ds + 1) // 2 if dl == 0 else 2 + (dl + 1) // 2
+            src_part, dst_part = src[1].at[k], dst[1].at[k]
+        else:
+            src_part = src[0].at[lead_src(dl), sub_src(ds), :]
+            dst_part = dst[0].at[lead_dst(dl), sub_dst(ds), :]
         return pltpu.make_async_remote_copy(
-            src_ref=src.at[lead_src(dl), sub_src(ds), :],
-            dst_ref=dst.at[lead_dst(dl), sub_dst(ds), :],
+            src_ref=src_part,
+            dst_ref=dst_part,
             send_sem=ss.at[i],
             recv_sem=rs.at[i],
             device_id=(a, b),
@@ -188,20 +208,20 @@
     for dl, ds in OFFSETS:
         a, b = c - dl, r - ds
         ok = inside(a, b) & ((a != r) | (b != c))
-        out = message(own_p, far_h, far_ss, far_rs, dl, ds, a, b)
+        out = message((own_p, side_p), (far_h, far_side), far_ss, far_rs, dl, ds, a, b)
         far_out.append((ok, out))
         pl.when(ok)(out.start)
         ok_in = inside(c + ds, r + dl) & ((c + ds != r) | (r + dl != c))
-        far_in.append((ok_in, message(own_p, far_h, far_ss, far_rs, dl, ds, r, c)))
+        far_in.append((ok_in, message((own_p, side_p), (far_h, far_side), far_ss, far_rs, dl, ds, r, c)))
     for dl, ds in OFFSETS:
         if dl or ds:
             a, b = r - dl, c - ds
             ok = inside(a, b)
-            out = message(own_q, near_h, near_ss, near_rs, dl, ds, a, b)
+            out = message((own_q, side_q), (near_h, near_side), near_ss, near_rs, dl, ds, a, b)
             near_out.append((ok, out))
             pl.when(ok)(out.start)
             near_in.append(
-                (inside(r + dl, c + ds), message(own_q, near_h, near_ss, near_rs, dl, ds, r, c))
+                (inside(r + dl, c + ds), message((own_q, side_q), (near_h, near_side), near_ss, near_rs, dl, ds, r, c))
             )
 
     for load in loads[1:]:
@@ -243,10 +263,23 @@
         for s in range(3):
             ref[s, parity, at] = line[pl.ds(first + s - 1, rows), :].astype(BF16)
 
-    def embed(patches, diag):
+    def embed(patches, sides, diag):
+        up, down = sides[0].astype(F32), sides[1].astype(F32)
         for h in range(6):
             first, last = (5, 8) if h == 0 else (0, 3) if h == 5 else (0, 8)
-            wide = jnp.dot(patches[h], diag, preferred_element_type=F32)
+            line = line_buf.at[h]
+            if 0 < h < 5:
+                line[PAD - 4 : PAD, :] = up[4 * h - 4 : 4 * h]
+                line[PAD : PAD + TILE, :] = patches[h, PAD : PAD + TILE, :].astype(F32)
+                line[PAD + TILE : PAD + TILE + 4, :] = down[4 * h - 4 : 4 * h]
+            else:
+                half = sides[2 if h == 0 else 3].astype(F32)
+                turned = pltpu.roll(half, 64, 1)
+                line[:PAD, :] = patches[h, :PAD, :].astype(F32)
+                line[PAD : PAD + 16, :] = turned if h == 0 else half
+                line[PAD + 16 : PAD + 32, :] = half if h == 0 else turned
+                line[PAD + TILE :, :] = patches[h, PAD + TILE :, :].astype(F32)
+            wide = jnp.dot(line[...].astype(BF16), diag, preferred_element_type=F32)
             for b in range(first, last):
                 at = h * BLK + b - 5
                 cells = wide[:, b * CH : (b + 1) * CH] + eb_ref[...]
@@ -301,7 +334,7 @@
     diag_q = block_diagonal(True)
     for ok, got_in in near_in:
         pl.when(ok)(got_in.wait_recv)
-    embed(near_h, diag_q)
+    embed(near_h, near_side, diag_q)
 
     def keep_own(m, h, value):
         f3[2 * m + h] = value
@@ -311,7 +344,7 @@
     diag_p = block_diagonal(False)
     for ok, got_in in far_in:
         pl.when(ok)(got_in.wait_recv)
-    embed(far_h, diag_p)
+    embed(far_h, far_side, diag_p)
 
     outs = []
 
@@ -441,6 +474,12 @@
             pltpu.VMEM((4, TILE, 128), BF16),
             pltpu.VMEM((6, TILE + 2 * PAD, 128), BF16),
             pltpu.VMEM((6, TILE + 2 * PAD, 128), BF16),
+            pltpu.VMEM((4, 16, 128), BF16),
+            pltpu.VMEM((4, 16, 128), BF16),
+            pltpu.VMEM((4, 16, 128), BF16),
+            pltpu.VMEM((4, 16, 128), BF16),
+            pltpu.VMEM((4, 16, 128), F32),
+            pltpu.VMEM((6, TILE + 2 * PAD, 128), F32),
             pltpu.VMEM((3, 2, 19, SUB, CH), BF16),
             pltpu.VMEM((3, 2, 18, SUB, CH), BF16),
             pltpu.VMEM((3, 2, 17, TILE, CH), BF16),

time: 30 us -> 29.8 us (level)
  no operation moved by 1% of the time
where the time goes in v5:
time: 29.8 us; the launch traced here: 29.6 us
  Pallas kernels  29 us (97%)
  between operations  0.64 us (2%)
    pallas_call x1, Pallas kernels, body(): pl.pallas_call(functools.partial(kernel, n), out_shape=shapes, in_specs=[...  27.4 us
    pallas_call x1, Pallas kernels, body(): pl.pallas_call(hand_over, out_shape=shapes, in_specs=[hbm, hbm], out_spec...  1.65 us

profile of v5, /device:TPU:1, one launch (start us, length us, event | category | flops | bytes accessed | tf_op | source)
XLA Modules:
  0.0 29.6 jit_solution(8028331921846457095)
XLA Ops:
  0.6 27.4 %shard_map.140 = (bf16[2,256]{1,0:T(2,128)(2,1)}, bf16[32,32,128]{2,1,0:T(8,128)(2,1)}) custom-call(f32[128,128]{1,0:T(8,128)} %x_hbm.1, bf16[16,128]{1,0:T(8,128)(2,1)} %ew_hbm.1, f32[1,128]{1,0:T(1,128)} %bitcast.10, bf16[3,1152,128]{2,1,0:T(8,128)(2,1)} %bitcast.6, f32[3,128]{1,0:T(4,128)} %cb_hbm.1, bf16[128,128]{1,0:T(8,128)(2,1)} %mw_hbm.1, ...), custom_call_target="tpu_custom_call" | custom-call | tf_op jit(solution)/shard_map/pallas_call | solution.py:465
  28.0 1.7 %shard_map.141 = (bf16[2,256]{1,0:T(2,128)(2,1)}, bf16[32,32,128]{2,1,0:T(8,128)(2,1)}) custom-call(bf16[2,256]{1,0:T(2,128)(2,1)} %get-tuple-element.4.lat_ref, bf16[32,32,128]{2,1,0:T(8,128)(2,1)} %get-tuple-element.5.sym_ref), custom_call_target="tpu_custom_call" | custom-call | tf_op jit(solution)/shard_map/pallas_call | solution.py:506
